TPU v7x, 256 devices: a whole 4x4x8 slice. The times are simulated.
256 devices in a mesh: region: 16 (over z, x_hi), feat: 4 (over x_lo, core), row: 4 (over y).
Axes of the slice: x: 4 (x_hi: 2, x_lo: 2; x = x_hi * 2 + x_lo), y: 4, z: 8, core: 2. Of those that a mesh axis runs over, the one named last changes fastest.
Arguments:
- samples: bfloat16 [524288, 128], P(('region', 'row')), may hold values from -6 to 6
- targets: bfloat16 [524288, 64], P(('region', 'row')), may hold values from -6 to 6
- member: int32 [524288], P(('region', 'row')), may hold values 0 or 1
- omega: bfloat16 [128, 4096], P(None, 'feat'), may hold values from -0.5 to 0.5
- phase: float32 [4096], P('feat'), may hold values from -3.140625 to 3.140625
- factors: float32 [65536, 1024], P(('region', 'feat')), may hold values from -0.08 to 5, as said below
- weights_init: float32 [65536, 64], P(('region', 'feat'), 'row'), may hold values from -3 to 3
- duals_init: float32 [65536, 64], P(('region', 'feat'), 'row'), may hold values from -2 to 2
- consensus_init: float32 [4096, 64], P('feat', 'row'), may hold values from -3 to 3
- penalty_init: float32 [16], P('region'), may hold values from 2 to 8
Outputs:
- weights: float32 [65536, 64], P(('region', 'feat'), 'row')
- duals: float32 [65536, 64], P(('region', 'feat'), 'row')
- consensus: float32 [4096, 64], P('feat', 'row')
- penalty: float32 [16, 3], P('region')
Inputs may be any that keep to these rules, and one draw needn't show every extreme that they name: factors: each 1024 x 1024 block is lower triangular, its diagonal between 3.5 and 5, its entries below the diagonal drawn independently, symmetric about zero and at most 0.08 in magnitude.
All inputs are finite; a program needn't handle non-finite values. No bound on the sum of `member` on one device may be relied on, other than what follows from the above.
Results may differ from a plain program's by a relative error of at most 0.006.
Values may be sent and summed in bfloat16 or wider, within the bound.
A program may use at most 128 MiB of HBM per device.

v0:
```python
import functools
import math

import jax
import jax.numpy as jnp
from jax import lax
from jax.experimental import pallas as pl
from jax.experimental.pallas import tpu as pltpu
from jax.sharding import PartitionSpec as P

ITERS = 3
CORES = 2
PARTS = 2
MESH = pl.DeviceIdType.MESH
INV_TURN = 1.0 / (2.0 * math.pi)
COS_TERMS = (0.99999921, -19.73898042, 64.9286585, -85.2716283, 58.79050663, -21.07110846)
F32 = jnp.float32
BF16 = jnp.bfloat16


def dot(a, b):
    return lax.dot_general(a, b, (((1,), (0,)), ((), ())), preferred_element_type=F32)


def dot_nt(a, b):
    return lax.dot_general(a, b, (((1,), (1,)), ((), ())), preferred_element_type=F32)


def feature_tile(scale, omega, phase, samples):
    turns = dot_nt(omega, samples) * INV_TURN + phase * INV_TURN
    rest = turns - jnp.round(turns)
    square = rest * rest
    value = scale * COS_TERMS[-1]
    for term in COS_TERMS[-2::-1]:
        value = value * square + scale * term
    return value.astype(BF16)


def invert(base, factor_ref, dinv_ref, n_ref, t_ref):
    size = factor_ref.shape[0]
    t_ref[...] = jnp.zeros_like(t_ref)
    powers, totals = [], []
    for start in range(0, size, base):
        rows = factor_ref[start : start + base, :]
        row = lax.broadcasted_iota(jnp.int32, rows.shape, 0) + start
        column = lax.broadcasted_iota(jnp.int32, rows.shape, 1)
        diagonal = jnp.sum(jnp.where(row == column, rows, 0.0), axis=1, keepdims=True)
        n_ref[start : start + base, :] = jnp.where(row > column, rows / diagonal, 0.0).astype(BF16)
        block = factor_ref[start : start + base, start : start + base]
        inner_row = lax.broadcasted_iota(jnp.int32, block.shape, 0)
        inner_column = lax.broadcasted_iota(jnp.int32, block.shape, 1)
        on = jnp.sum(jnp.where(inner_row == inner_column, block, 0.0), axis=0, keepdims=True)
        dinv_ref[:, start : start + base] = 1.0 / on
        power = -n_ref[start : start + base, start : start + base].astype(F32)
        powers.append(power)
        totals.append(power)
    reach = 2
    while reach < base:
        for index in range(len(powers)):
            low = powers[index].astype(BF16)
            square = dot(low, low)
            low = square.astype(BF16)
            totals[index] = totals[index] + square + dot(totals[index].astype(BF16), low)
            powers[index] = square
        reach *= 2
    for index, start in enumerate(range(0, size, base)):
        t_ref[start : start + base, start : start + base] = totals[index].astype(BF16)
    width = base
    while width < size:
        for start in range(0, size, 2 * width):
            top = slice(start, start + width)
            bottom = slice(start + width, start + 2 * width)
            below = n_ref[bottom, top]
            first = below.astype(F32) + dot(below, t_ref[top, top])
            second = first + dot(t_ref[bottom, bottom], first.astype(BF16))
            t_ref[bottom, top] = (-second).astype(BF16)
        width *= 2


def admm_kernel(
    sizes,
    offset,
    scale,
    penalty_ref,
    samples_hbm,
    targets_hbm,
    member_hbm,
    omega_ref,
    phase_ref,
    factor_hbm,
    weights_ref,
    duals_ref,
    consensus_ref,
    out_ref,
    history_ref,
    factor_ref,
    dinv_ref,
    strict_ref,
    solve_ref,
    samples_ref,
    targets_ref,
    member_ref,
    far_omega_ref,
    far_phase_ref,
    turned_ref,
    column_ref,
    feat_ref,
    coarse_ref,
    acc_ref,
    part_ref,
    other_ref,
    resid_ref,
    gfar_ref,
    gside_ref,
    gsum_ref,
    gsend_ref,
    grow_ref,
    reg_ref,
    gap_ref,
    load_sem,
    omega_send,
    omega_recv,
    crow_send,
    crow_recv,
    cside_send,
    cside_recv,
    core_send,
    core_recv,
    gside_send,
    gside_recv,
    grow_send,
    grow_recv,
    reg_send,
    reg_recv,
    gap_send,
    gap_recv,
):
    n_region, n_feat, n_row = sizes
    narrow, width = weights_ref.shape
    outputs = n_row * narrow
    count = feat_ref.shape[2]
    chunk = min(1024, count)
    chunks = count // chunk
    piece_width = width // PARTS
    tile, broad = min(256, piece_width), min(512, piece_width)
    region, feat, row = lax.axis_index("region"), lax.axis_index("feat"), lax.axis_index("row")
    group = n_feat * n_row
    place = feat * n_row + row
    side = (region, lax.rem(feat + CORES, n_feat), row)
    core = (region, feat + 1 - 2 * lax.rem(feat, CORES), row)

    def row_peer(k):
        return (region, feat, lax.rem(row + k, n_row))

    def region_peer(k):
        return (lax.rem(region + k, n_region), feat, row)

    def group_peer(k):
        other = lax.rem(place + k, group)
        return (region, other // n_row, lax.rem(other, n_row))

    def remote(src, dst, send, recv, device):
        return pltpu.make_async_remote_copy(
            src_ref=src, dst_ref=dst, send_sem=send, recv_sem=recv,
            device_id=device, device_id_type=MESH,
        )

    first = pl.multiple_of((feat // CORES) * count, 128)
    span = pl.ds(first, count)
    loads = [
        pltpu.make_async_copy(samples_hbm.at[span], samples_ref, load_sem.at[0]),
        pltpu.make_async_copy(targets_hbm.at[:, span], targets_ref, load_sem.at[1]),
        pltpu.make_async_copy(member_hbm.at[:, span], member_ref, load_sem.at[2]),
        pltpu.make_async_copy(factor_hbm, factor_ref, load_sem.at[3]),
    ]
    for load in loads:
        load.start()

    barrier = pltpu.get_barrier_semaphore()
    for k in range(1, group):
        pl.semaphore_signal(barrier, inc=1, device_id=group_peer(k), device_id_type=MESH)
    for k in range(1, n_region):
        pl.semaphore_signal(barrier, inc=1, device_id=region_peer(k), device_id_type=MESH)

    trips = (width // tile) * chunks

    def prepare(omega, phase):
        turned_ref[...] = omega.astype(F32).T.astype(BF16)
        for j in range(width // tile):
            span = slice(j * tile, (j + 1) * tile)
            level = lax.broadcasted_iota(jnp.int32, (tile, tile), 0)
            across = lax.broadcasted_iota(jnp.int32, (tile, tile), 1)
            only = jnp.where(level == across, phase[:, span], 0.0)
            column_ref[span, :] = jnp.sum(only, axis=1, keepdims=True)

    def fill(half, low, high):
        def step(i, carry):
            down = pl.multiple_of((i // chunks) * tile, tile)
            right = pl.multiple_of((i % chunks) * chunk, chunk)
            feat_ref[half, pl.ds(down, tile), pl.ds(right, chunk)] = feature_tile(
                scale,
                turned_ref[pl.ds(down, tile), :],
                column_ref[pl.ds(down, tile), :],
                samples_ref[pl.ds(right, chunk), :],
            )
            return carry

        lax.fori_loop(low, high, step, 0)

    weights, duals, consensus = weights_ref[...], duals_ref[...], consensus_ref[...]
    rho = jnp.full((1, 128), penalty_ref[0], F32)
    history = jnp.zeros((1, 128), F32)
    lane = lax.broadcasted_iota(jnp.int32, (1, 128), 1)
    loads[0].wait()
    prepare(omega_ref[...], phase_ref[...])
    fill(0, 0, trips // 2)
    pl.semaphore_wait(barrier, group - 1 + n_region - 1)
    sends = []

    for t in range(ITERS):
        coarse_ref[t, 0, row] = weights.astype(BF16)
        mine = coarse_ref.at[t, 0, row]
        for k in range(1, n_row):
            copy = remote(mine, mine, crow_send.at[t, k], crow_recv.at[t, k], row_peer(k))
            copy.start()
            sends.append(copy)
        copy = remote(
            mine, coarse_ref.at[t, 1, row], cside_send.at[t, 0], cside_recv.at[t, 0], side
        )
        copy.start()
        sends.append(copy)

        if t > 0:
            duals, consensus = finish_region(t - 1)
        else:
            exchange = [
                remote(omega_ref, far_omega_ref, omega_send.at[0], omega_recv.at[0], side),
                remote(phase_ref, far_phase_ref, omega_send.at[1], omega_recv.at[1], side),
            ]
            for copy in exchange:
                copy.start()
                sends.append(copy)
            fill(0, trips // 2, trips)

        for k in range(1, n_row):
            source = lax.rem(row - k + n_row, n_row)
            piece = coarse_ref.at[t, 0, source]
            remote(piece, piece, crow_send.at[t, k], crow_recv.at[t, k], side).wait_recv()
            copy = remote(
                piece, coarse_ref.at[t, 1, source], cside_send.at[t, k], cside_recv.at[t, k], side
            )
            copy.start()
            sends.append(copy)
        if t == 0:
            for copy in exchange:
                copy.wait_recv()
            prepare(far_omega_ref[...], far_phase_ref[...])
            fill(1, 0, trips)
            loads[1].wait()
            loads[2].wait()
        near = coarse_ref[t, 0].reshape(outputs, width)
        for j in range(chunks):
            span = slice(j * chunk, (j + 1) * chunk)
            acc_ref[:, span] = dot(near, feat_ref[0, :, span])
        for k in range(n_row):
            source = lax.rem(row - k + n_row, n_row)
            piece = coarse_ref.at[t, 1, source]
            remote(piece, piece, cside_send.at[t, k], cside_recv.at[t, k], side).wait_recv()
        far = coarse_ref[t, 1].reshape(outputs, width)
        for j in range(chunks):
            span = slice(j * chunk, (j + 1) * chunk)
            part = acc_ref[:, span] + dot(far, feat_ref[1, :, span])
            acc_ref[:, span] = part
            part_ref[t, j] = part.astype(BF16)
            copy = remote(
                part_ref.at[t, j], other_ref.at[t, j], core_send.at[t, j], core_recv.at[t, j], core
            )
            copy.start()
            sends.append(copy)
        for j in range(chunks):
            span = slice(j * chunk, (j + 1) * chunk)
            piece = other_ref.at[t, j]
            remote(piece, piece, core_send.at[t, j], core_recv.at[t, j], core).wait_recv()
            predicted = acc_ref[:, span] + other_ref[t, j].astype(F32)
            gap_value = predicted - targets_ref[:, span].astype(F32)
            resid_ref[:, span] = (member_ref[:, span].astype(F32) * gap_value).astype(BF16)

        for p in range(PARTS):
            for j in range(piece_width // broad):
                inside = slice(j * broad, (j + 1) * broad)
                span = slice(p * piece_width + j * broad, p * piece_width + (j + 1) * broad)
                value = dot_nt(resid_ref[...], feat_ref[1, span, :])
                gfar_ref[t, p, :, :, inside] = value.astype(BF16).reshape(n_row, narrow, broad)
            copy = remote(
                gfar_ref.at[t, p], gside_ref.at[t, p], gside_send.at[t, p], gside_recv.at[t, p],
                side,
            )
            copy.start()
            sends.append(copy)
        for p in range(PARTS):
            for j in range(piece_width // broad):
                inside = slice(j * broad, (j + 1) * broad)
                span = slice(p * piece_width + j * broad, p * piece_width + (j + 1) * broad)
                value = dot_nt(resid_ref[...], feat_ref[0, span, :])
                gsum_ref[p, :, :, inside] = value.reshape(n_row, narrow, broad)
            piece = gside_ref.at[t, p]
            remote(piece, piece, gside_send.at[t, p], gside_recv.at[t, p], side).wait_recv()
            for k in range(1, n_row):
                target = lax.rem(row + k, n_row)
                value = gsum_ref[p, target] + gside_ref[t, p, target].astype(F32)
                gsend_ref[t, p, k] = value.astype(BF16)
                copy = remote(
                    gsend_ref.at[t, p, k], grow_ref.at[t, p, k], grow_send.at[t, p, k],
                    grow_recv.at[t, p, k], row_peer(k),
                )
                copy.start()
                sends.append(copy)
        if t > 0:
            rho, duals, history = finish_gap(t - 1, rho, duals, history)
        else:
            loads[3].wait()
            invert(min(256, width), factor_ref, dinv_ref, strict_ref, solve_ref)
        dinv = dinv_ref[...]
        scalar = rho[:, :1]
        gradient = []
        for p in range(PARTS):
            value = gsum_ref[p, row] + gside_ref[t, p, row].astype(F32)
            for k in range(1, n_row):
                piece = grow_ref.at[t, p, k]
                remote(
                    piece, piece, grow_send.at[t, p, k], grow_recv.at[t, p, k], side
                ).wait_recv()
                value = value + grow_ref[t, p, k].astype(F32)
            gradient.append(value)
        right = scalar * (weights - consensus + duals) + jnp.concatenate(gradient, axis=1)
        forward = right * dinv
        forward = forward + dot_nt(forward.astype(BF16), solve_ref[...])
        backward = (forward + dot(forward.astype(BF16), solve_ref[...])) * dinv
        weights = weights - backward

        reg_ref[t, region, :narrow] = scalar * (weights + duals)
        reg_ref[t, region, narrow:] = jnp.broadcast_to(scalar, (8, width))
        mine = reg_ref.at[t, region]
        for k in range(1, n_region):
            copy = remote(mine, mine, reg_send.at[t, k], reg_recv.at[t, k], region_peer(k))
            copy.start()
            sends.append(copy)

        def finish_region(s, weights=weights, duals=duals, consensus=consensus):
            for k in range(1, n_region):
                source = lax.rem(region - k + n_region, n_region)
                piece = reg_ref.at[s, source]
                remote(
                    piece, piece, reg_send.at[s, k], reg_recv.at[s, k], region_peer(k)
                ).wait_recv()
            total = reg_ref[s, 0]
            for r in range(1, n_region):
                total = total + reg_ref[s, r]
            updated = total[:narrow] / total[narrow : narrow + 1]
            gap = jnp.sum(jnp.square(weights - updated), keepdims=True).reshape(1, 1)
            drift = jnp.sum(jnp.square(updated - consensus), keepdims=True).reshape(1, 1)
            level = lax.broadcasted_iota(jnp.int32, (8, 128), 0)
            gap_ref[s, place] = jnp.where(level == 0, gap, drift)
            mine = gap_ref.at[s, place]
            for k in range(1, group):
                copy = remote(mine, mine, gap_send.at[s, k], gap_recv.at[s, k], group_peer(k))
                copy.start()
                sends.append(copy)
            return duals + weights - updated, updated

        def finish_gap(s, rho, duals, history):
            for k in range(1, group):
                source = lax.rem(place - k + group, group)
                piece = gap_ref.at[s, source]
                remote(
                    piece, piece, gap_send.at[s, k], gap_recv.at[s, k], group_peer(k)
                ).wait_recv()
            total = jnp.sum(gap_ref[s], axis=0)
            gap, drift = total[0:1], total[1:2]
            drift = rho * rho * drift
            renewed = rho * jnp.sqrt((gap + offset) / (drift + offset))
            duals = duals * (rho / renewed)[:, :1]
            return renewed, duals, jnp.where(lane == s, renewed, history)

    duals, consensus = finish_region(ITERS - 1)
    rho, duals, history = finish_gap(ITERS - 1, rho, duals, history)
    out_ref[0] = weights
    out_ref[1] = duals
    out_ref[2] = consensus
    history_ref[...] = history
    for copy in sends:
        copy.wait_send()


def admm(sizes, offset, scale, penalty, samples, targets, member, omega, phase, factors, *state):
    n_region, n_feat, n_row = sizes
    narrow, width = state[0].shape
    outputs = n_row * narrow
    inputs = omega.shape[0]
    count = samples.shape[0] // (n_feat // CORES)
    chunk = min(1024, count)
    chunks = count // chunk
    group = n_feat * n_row
    part = (n_row, narrow, width // PARTS)
    vmem = pl.BlockSpec(memory_space=pltpu.VMEM)
    hbm = pl.BlockSpec(memory_space=pl.ANY)
    dma = pltpu.SemaphoreType.DMA
    return pl.pallas_call(
        functools.partial(admm_kernel, sizes, offset, scale),
        in_specs=[pl.BlockSpec(memory_space=pltpu.SMEM), hbm, hbm, hbm] + [vmem, vmem, hbm, vmem, vmem, vmem],
        out_specs=[vmem, vmem],
        out_shape=[
            jax.ShapeDtypeStruct((3, narrow, width), F32),
            jax.ShapeDtypeStruct((1, 128), F32),
        ],
        scratch_shapes=[
            pltpu.VMEM((width, width), F32),
            pltpu.VMEM((1, width), F32),
            pltpu.VMEM((width, width), BF16),
            pltpu.VMEM((width, width), BF16),
            pltpu.VMEM((count, inputs), BF16),
            pltpu.VMEM((outputs, count), BF16),
            pltpu.VMEM((1, count), jnp.int32),
            pltpu.VMEM((inputs, width), BF16),
            pltpu.VMEM((1, width), F32),
            pltpu.VMEM((width, inputs), BF16),
            pltpu.VMEM((width, 1), F32),
            pltpu.VMEM((2, width, count), BF16),
            pltpu.VMEM((ITERS, 2, n_row, narrow, width), BF16),
            pltpu.VMEM((outputs, count), F32),
            pltpu.VMEM((ITERS, chunks, outputs, chunk), BF16),
            pltpu.VMEM((ITERS, chunks, outputs, chunk), BF16),
            pltpu.VMEM((outputs, count), BF16),
            pltpu.VMEM((ITERS, PARTS) + part, BF16),
            pltpu.VMEM((ITERS, PARTS) + part, BF16),
            pltpu.VMEM((PARTS,) + part, F32),
            pltpu.VMEM((ITERS, PARTS) + part, BF16),
            pltpu.VMEM((ITERS, PARTS) + part, BF16),
            pltpu.VMEM((ITERS, n_region, narrow + 8, width), F32),
            pltpu.VMEM((ITERS, group, 8, 128), F32),
            dma((4,)),
            dma((2,)),
            dma((2,)),
            dma((ITERS, n_row)),
            dma((ITERS, n_row)),
            dma((ITERS, n_row)),
            dma((ITERS, n_row)),
            dma((ITERS, chunks)),
            dma((ITERS, chunks)),
            dma((ITERS, PARTS)),
            dma((ITERS, PARTS)),
            dma((ITERS, PARTS, n_row)),
            dma((ITERS, PARTS, n_row)),
            dma((ITERS, n_region)),
            dma((ITERS, n_region)),
            dma((ITERS, group)),
            dma((ITERS, group)),
        ],
        compiler_params=pltpu.CompilerParams(
            collective_id=0, has_side_effects=True, vmem_limit_bytes=56 * 2**20
        ),
        name="admm",
    )(penalty, samples, targets, member, omega, phase, factors, *state)


def per_device(
    sizes,
    samples,
    targets,
    member,
    omega,
    phase,
    factors,
    weights_init,
    duals_init,
    consensus_init,
    penalty_init,
):
    n_region, n_feat, n_row = sizes
    total_features = n_feat * omega.shape[1]
    total_outputs = targets.shape[1]
    offset = 0.01 * total_features * total_outputs
    scale = math.sqrt(2.0 / total_features)
    final, history = admm(
        sizes, offset, scale, penalty_init, samples, targets.T, member[None, :], omega,
        phase[None, :], factors, weights_init.T, duals_init.T, consensus_init.T,
    )
    return (final[0].T, final[1].T, final[2].T, history[:, :ITERS])


def solution(mesh):
    sizes = (mesh.shape["region"], mesh.shape["feat"], mesh.shape["row"])
    return jax.shard_map(
        functools.partial(per_device, sizes),
        mesh=mesh,
        in_specs=(
            P(("region", "row"), None),
            P(("region", "row"), None),
            P(("region", "row")),
            P(None, "feat"),
            P("feat"),
            P(("region", "feat"), None),
            P(("region", "feat"), "row"),
            P(("region", "feat"), "row"),
            P("feat", "row"),
            P("region"),
        ),
        out_specs=(
            P(("region", "feat"), "row"),
            P(("region", "feat"), "row"),
            P("feat", "row"),
            P("region", None),
        ),
        check_vma=False,
    )
```

profile of v0, /device:TPU:65, one launch (start us, length us, event | category | flops | bytes accessed | tf_op | source)
XLA Modules:
  0.0 212.3 jit_solution(18052198518796438115)
XLA Ops:
  1.3 208.3 %admm.1 = (f32[3,16,1024]{2,1,0:T(8,128)}, f32[1,128]{1,0:T(1,128)}) custom-call(f32[1]{0:T(128)S(6)} %copy.15.penalty_ref, bf16[8192,128]{1,0:T(8,128)(2,1)} %samples_hbm.1, bf16[64,8192]{1,0:T(8,128)(2,1)} %bitcast.19, s32[1,8192]{1,0:T(1,128)} %bitcast.23, bf16[128,1024]{1,0:T(8,128)(2,1)} %omega_ref.1, f32[1,1024]{1,0:T(1,128)} %bitcast.24, ...), custom_call_target="tpu_custom_call" | custom-call | tf_op jit(solution)/shard_map/admm/pallas_call | solution.py:408
  209.6 1.6 slice_bitcast_fusion
  211.2 1.1 copy.16
where the time goes:
time: 212 us
  Pallas kernels  208 us (98%)
  local copies, waits for them, and re-layouts  2.7 us (1%)
    pallas_call x1, Pallas kernels, admm(): pl.pallas_call(functools.partial(admm_kernel, sizes, offset, scale), in_s...  208 us

commit v1 on v0

--- a/solution.py
+++ b/solution.py
@@ -115,7 +115,9 @@
     gsum_ref,
     gsend_ref,
     grow_ref,
-    reg_ref,
+    rs_send_ref,
+    rs_recv_ref,
+    mean_ref,
     gap_ref,
     load_sem,
     omega_send,
@@ -130,14 +132,17 @@
     gside_recv,
     grow_send,
     grow_recv,
-    reg_send,
-    reg_recv,
+    rs_send,
+    rs_recv,
+    mean_send,
+    mean_recv,
     gap_send,
     gap_recv,
 ):
     n_region, n_feat, n_row = sizes
     narrow, width = weights_ref.shape
     outputs = n_row * narrow
+    lanes = width // 128
     count = feat_ref.shape[2]
     chunk = min(1024, count)
     chunks = count // chunk
@@ -230,9 +235,7 @@
         copy.start()
         sends.append(copy)
 
-        if t > 0:
-            duals, consensus = finish_region(t - 1)
-        else:
+        if t == 0:
             exchange = [
                 remote(omega_ref, far_omega_ref, omega_send.at[0], omega_recv.at[0], side),
                 remote(phase_ref, far_phase_ref, omega_send.at[1], omega_recv.at[1], side),
@@ -277,6 +280,8 @@
             )
             copy.start()
             sends.append(copy)
+        if t > 0:
+            share_mean(t - 1)
         for j in range(chunks):
             span = slice(j * chunk, (j + 1) * chunk)
             piece = other_ref.at[t, j]
@@ -298,6 +303,8 @@
             copy.start()
             sends.append(copy)
         for p in range(PARTS):
+            if t > 0 and p == PARTS - 1:
+                duals, consensus = finish_region(t - 1)
             for j in range(piece_width // broad):
                 inside = slice(j * broad, (j + 1) * broad)
                 span = slice(p * piece_width + j * broad, p * piece_width + (j + 1) * broad)
@@ -338,25 +345,52 @@
         backward = (forward + dot(forward.astype(BF16), solve_ref[...])) * dinv
         weights = weights - backward
 
-        reg_ref[t, region, :narrow] = scalar * (weights + duals)
-        reg_ref[t, region, narrow:] = jnp.broadcast_to(scalar, (8, width))
-        mine = reg_ref.at[t, region]
+        total = scalar * (weights + duals)
+        for c in range(n_region):
+            down, right = 8 * (c // lanes), 128 * (c % lanes)
+            rs_send_ref[t, c, :8] = total[down : down + 8, right : right + 128]
+            rs_send_ref[t, c, 8:] = jnp.broadcast_to(scalar, (8, 128))
+        rs_recv_ref[t, region] = rs_send_ref[t, region]
         for k in range(1, n_region):
-            copy = remote(mine, mine, reg_send.at[t, k], reg_recv.at[t, k], region_peer(k))
+            owner = lax.rem(region + k, n_region)
+            copy = remote(
+                rs_send_ref.at[t, owner, pl.ds(0, 9)], rs_recv_ref.at[t, region, pl.ds(0, 9)],
+                rs_send.at[t, k], rs_recv.at[t, k], region_peer(k),
+            )
             copy.start()
             sends.append(copy)
+
+        def share_mean(s):
+            for k in range(1, n_region):
+                source = lax.rem(region - k + n_region, n_region)
+                piece = rs_recv_ref.at[s, source, pl.ds(0, 9)]
+                remote(
+                    piece, piece, rs_send.at[s, k], rs_recv.at[s, k], region_peer(k)
+                ).wait_recv()
+            total = rs_recv_ref[s, 0, :9]
+            for r in range(1, n_region):
+                total = total + rs_recv_ref[s, r, :9]
+            mean_ref[s, region] = total[:8] / total[8:9]
+            mine = mean_ref.at[s, region]
+            for k in range(1, n_region):
+                copy = remote(mine, mine, mean_send.at[s, k], mean_recv.at[s, k], region_peer(k))
+                copy.start()
+                sends.append(copy)
 
         def finish_region(s, weights=weights, duals=duals, consensus=consensus):
             for k in range(1, n_region):
                 source = lax.rem(region - k + n_region, n_region)
-                piece = reg_ref.at[s, source]
+                piece = mean_ref.at[s, source]
                 remote(
-                    piece, piece, reg_send.at[s, k], reg_recv.at[s, k], region_peer(k)
+                    piece, piece, mean_send.at[s, k], mean_recv.at[s, k], region_peer(k)
                 ).wait_recv()
-            total = reg_ref[s, 0]
-            for r in range(1, n_region):
-                total = total + reg_ref[s, r]
-            updated = total[:narrow] / total[narrow : narrow + 1]
+            updated = jnp.concatenate(
+                [
+                    jnp.concatenate([mean_ref[s, h * lanes + j] for j in range(lanes)], axis=1)
+                    for h in range(narrow // 8)
+                ],
+                axis=0,
+            )
             gap = jnp.sum(jnp.square(weights - updated), keepdims=True).reshape(1, 1)
             drift = jnp.sum(jnp.square(updated - consensus), keepdims=True).reshape(1, 1)
             level = lax.broadcasted_iota(jnp.int32, (8, 128), 0)
@@ -382,6 +416,7 @@
             duals = duals * (rho / renewed)[:, :1]
             return renewed, duals, jnp.where(lane == s, renewed, history)
 
+    share_mean(ITERS - 1)
     duals, consensus = finish_region(ITERS - 1)
     rho, duals, history = finish_gap(ITERS - 1, rho, duals, history)
     out_ref[0] = weights
@@ -436,7 +471,9 @@
             pltpu.VMEM((PARTS,) + part, F32),
             pltpu.VMEM((ITERS, PARTS) + part, BF16),
             pltpu.VMEM((ITERS, PARTS) + part, BF16),
-            pltpu.VMEM((ITERS, n_region, narrow + 8, width), F32),
+            pltpu.VMEM((ITERS, n_region, 16, 128), F32),
+            pltpu.VMEM((ITERS, n_region, 16, 128), F32),
+            pltpu.VMEM((ITERS, n_region, 8, 128), F32),
             pltpu.VMEM((ITERS, group, 8, 128), F32),
             dma((4,)),
             dma((2,)),
@@ -451,6 +488,8 @@
             dma((ITERS, PARTS)),
             dma((ITERS, PARTS, n_row)),
             dma((ITERS, PARTS, n_row)),
+            dma((ITERS, n_region)),
+            dma((ITERS, n_region)),
             dma((ITERS, n_region)),
             dma((ITERS, n_region)),
             dma((ITERS, group)),

time: 212 us -> 120 us (0.57)
  the two profiles are of different devices: /device:TPU:65 before, /device:TPU:1 now
where the time goes in v1:
time: 120 us
  Pallas kernels  116 us (97%)
  local copies, waits for them, and re-layouts  2.7 us (2%)
  between operations  1.29 us (1%)
    pallas_call x1, Pallas kernels, admm(): pl.pallas_call(functools.partial(admm_kernel, sizes, offset, scale), in_s...  116 us

profile of v1, /device:TPU:1, one launch (start us, length us, event | category | flops | bytes accessed | tf_op | source)
XLA Modules:
  0.0 119.8 jit_solution(8417812192742216801)
XLA Ops:
  1.3 115.8 %admm.1 = (f32[3,16,1024]{2,1,0:T(8,128)}, f32[1,128]{1,0:T(1,128)}) custom-call(f32[1]{0:T(128)S(6)} %copy.15.penalty_ref, bf16[8192,128]{1,0:T(8,128)(2,1)} %samples_hbm.1, bf16[64,8192]{1,0:T(8,128)(2,1)} %bitcast.19, s32[1,8192]{1,0:T(1,128)} %bitcast.23, bf16[128,1024]{1,0:T(8,128)(2,1)} %omega_ref.1, f32[1,1024]{1,0:T(1,128)} %bitcast.24, ...), custom_call_target="tpu_custom_call" | custom-call | tf_op jit(solution)/shard_map/admm/pallas_call | solution.py:443
  117.1 1.6 %slice_bitcast_fusion = (f32[1024,16]{0,1:T(8,128)}, f32[1024,16]{0,1:T(8,128)}, f32[1024,16]{0,1:T(8,128)}) fusion(f32[3,16,1024]{2,1,0:T(8,128)} %get-tuple-element.6), kind=kLoop, calls=%fused_computation | loop fusion | bytes 393216 | tf_op jit(solution)/shard_map/transpose | solution.py:527
  118.7 1.1 copy.16

commit v2 on v1

v2 whole, which is shorter than its diff:
```python
import functools
import math

import jax
import jax.numpy as jnp
from jax import lax
from jax.experimental import pallas as pl
from jax.experimental.pallas import tpu as pltpu
from jax.sharding import PartitionSpec as P

ITERS = 3
CORES = 2
PARTS = 2
CHUNK = 2048
MESH = pl.DeviceIdType.MESH
INV_TURN = 1.0 / (2.0 * math.pi)
WAVE_GAIN, WAVE_MIDDLE, WAVE_LAST = 71.848585, -0.5703125, 0.08740234375
F32 = jnp.float32
BF16 = jnp.bfloat16


def dot(a, b):
    return lax.dot_general(a, b, (((1,), (0,)), ((), ())), preferred_element_type=F32)


def dot_nt(a, b):
    return lax.dot_general(a, b, (((1,), (1,)), ((), ())), preferred_element_type=F32)


def feature_tile(omega, phase, samples):
    turns = dot_nt(omega, samples) + phase
    rest = (0.25 - jnp.abs(turns - jnp.round(turns))).astype(BF16)
    square = rest * rest
    value = (square + jnp.asarray(WAVE_MIDDLE, BF16)) * square + jnp.asarray(WAVE_LAST, BF16)
    return value * rest


def invert(base, factor_ref, dinv_ref, n_ref, t_ref):
    size = factor_ref.shape[0]
    t_ref[...] = jnp.zeros_like(t_ref)
    powers, totals = [], []
    for start in range(0, size, base):
        rows = factor_ref[start : start + base, :]
        row = lax.broadcasted_iota(jnp.int32, rows.shape, 0) + start
        column = lax.broadcasted_iota(jnp.int32, rows.shape, 1)
        diagonal = jnp.sum(jnp.where(row == column, rows, 0.0), axis=1, keepdims=True)
        n_ref[start : start + base, :] = jnp.where(row > column, rows / diagonal, 0.0).astype(BF16)
        block = factor_ref[start : start + base, start : start + base]
        inner_row = lax.broadcasted_iota(jnp.int32, block.shape, 0)
        inner_column = lax.broadcasted_iota(jnp.int32, block.shape, 1)
        on = jnp.sum(jnp.where(inner_row == inner_column, block, 0.0), axis=0, keepdims=True)
        dinv_ref[:, start : start + base] = 1.0 / on
        power = -n_ref[start : start + base, start : start + base].astype(F32)
        powers.append(power)
        totals.append(power)
    reach = 2
    while reach < base:
        for index in range(len(powers)):
            low = powers[index].astype(BF16)
            square = dot(low, low)
            low = square.astype(BF16)
            totals[index] = totals[index] + square + dot(totals[index].astype(BF16), low)
            powers[index] = square
        reach *= 2
    for index, start in enumerate(range(0, size, base)):
        t_ref[start : start + base, start : start + base] = totals[index].astype(BF16)
    width = base
    while width < size:
        for start in range(0, size, 2 * width):
            top = slice(start, start + width)
            bottom = slice(start + width, start + 2 * width)
            below = n_ref[bottom, top]
            first = below.astype(F32) + dot(below, t_ref[top, top])
            second = first + dot(t_ref[bottom, bottom], first.astype(BF16))
            t_ref[bottom, top] = (-second).astype(BF16)
        width *= 2


def admm_kernel(
    sizes,
    offset,
    scale,
    penalty_ref,
    samples_hbm,
    targets_hbm,
    member_hbm,
    omega_hbm,
    phase_hbm,
    factor_hbm,
    weights_hbm,
    duals_hbm,
    consensus_hbm,
    out_hbm,
    factor_ref,
    dinv_ref,
    strict_ref,
    solve_ref,
    samples_ref,
    targets_ref,
    member_ref,
    omega_ref,
    phase_ref,
    state_ref,
    feat_ref,
    flip_ref,
    coarse_ref,
    acc_ref,
    part_ref,
    other_ref,
    resid_ref,
    gfar_ref,
    gside_ref,
    gown_ref,
    gsend_ref,
    grow_ref,
    rs_send_ref,
    rs_recv_ref,
    mean_ref,
    gap_ref,
    load_sem,
    store_sem,
    omega_send,
    omega_recv,
    phase_send,
    phase_recv,
    crow_send,
    crow_recv,
    cside_send,
    cside_recv,
    core_send,
    core_recv,
    gside_send,
    gside_recv,
    grow_send,
    grow_recv,
    rs_send,
    rs_recv,
    mean_send,
    mean_recv,
    gap_send,
    gap_recv,
):
    n_region, n_feat, n_row = sizes
    narrow, width = weights_hbm.shape
    outputs = n_row * narrow
    lanes = width // 128
    inputs = omega_hbm.shape[0]
    gain = scale * WAVE_GAIN
    count = feat_ref.shape[2]
    chunk = min(CHUNK, count)
    chunks = count // chunk
    piece_width = width // PARTS
    tile = min(512, piece_width)
    tiles = width // tile
    region, feat, row = lax.axis_index("region"), lax.axis_index("feat"), lax.axis_index("row")
    group = n_feat * n_row
    place = feat * n_row + row
    side = (region, lax.rem(feat + CORES, n_feat), row)
    core = (region, feat + 1 - 2 * lax.rem(feat, CORES), row)

    def row_peer(k):
        return (region, feat, lax.rem(row + k, n_row))

    def region_peer(k):
        return (lax.rem(region + k, n_region), feat, row)

    def far_peer(k):
        return (region, lax.rem(feat + CORES, n_feat), lax.rem(row + k, n_row))

    def group_peer(k):
        other = lax.rem(place + k, group)
        return (region, other // n_row, lax.rem(other, n_row))

    def remote(src, dst, send, recv, device):
        return pltpu.make_async_remote_copy(
            src_ref=src, dst_ref=dst, send_sem=send, recv_sem=recv,
            device_id=device, device_id_type=MESH,
        )

    first = pl.multiple_of((feat // CORES) * count, 128)
    span = pl.ds(first, count)
    loads = [
        pltpu.make_async_copy(samples_hbm.at[span], samples_ref.at[:, :inputs], load_sem.at[0]),
        pltpu.make_async_copy(omega_hbm, omega_ref.at[0], load_sem.at[1]),
        pltpu.make_async_copy(phase_hbm, phase_ref.at[0], load_sem.at[2]),
        pltpu.make_async_copy(weights_hbm, state_ref.at[0], load_sem.at[3]),
        pltpu.make_async_copy(duals_hbm, state_ref.at[1], load_sem.at[4]),
        pltpu.make_async_copy(consensus_hbm, state_ref.at[2], load_sem.at[5]),
        pltpu.make_async_copy(targets_hbm.at[:, span], targets_ref, load_sem.at[6]),
        pltpu.make_async_copy(member_hbm.at[:, span], member_ref, load_sem.at[7]),
        pltpu.make_async_copy(factor_hbm, factor_ref, load_sem.at[8]),
    ]
    for load in loads[:6]:
        load.start()

    barrier = pltpu.get_barrier_semaphore()
    for k in range(1, group):
        pl.semaphore_signal(barrier, inc=1, device_id=group_peer(k), device_id_type=MESH)
    for k in range(1, n_region):
        pl.semaphore_signal(barrier, inc=1, device_id=region_peer(k), device_id_type=MESH)

    def column_of(line):
        pieces = []
        for j in range(tile // 128):
            level = lax.broadcasted_iota(jnp.int32, (128, 128), 0)
            across = lax.broadcasted_iota(jnp.int32, (128, 128), 1)
            only = jnp.where(level == across, line[:, 128 * j : 128 * (j + 1)], 0.0)
            pieces.append(jnp.sum(only, axis=1, keepdims=True))
        return jnp.concatenate(pieces, axis=0)

    def omega_piece(i):
        span = pl.ds(pl.multiple_of(i * tile, tile), tile)
        return remote(
            omega_ref.at[0, :, span], omega_ref.at[1, :, span], omega_send.at[i], omega_recv.at[i],
            side,
        )

    def phase_copy():
        return remote(phase_ref.at[0], phase_ref.at[1], phase_send.at[0], phase_recv.at[0], side)

    def near_copies(t):
        mine = coarse_ref.at[t, 0, row]
        return [
            remote(mine, mine, crow_send.at[t], crow_recv.at[t], row_peer(k))
            for k in range(1, n_row)
        ]

    def far_copies(t):
        mine, there = coarse_ref.at[t, 0, row], coarse_ref.at[t, 1, row]
        return [
            remote(mine, there, cside_send.at[t], cside_recv.at[t], far_peer(k))
            for k in range(n_row)
        ]

    def arrived(pieces, semaphore):
        remote(pieces, pieces, semaphore, semaphore, side).wait_recv()

    def sent(pieces, semaphore):
        remote(pieces, pieces, semaphore, semaphore, side).wait_send()

    def core_copy(t, j):
        return remote(
            part_ref.at[t, j], other_ref.at[t, j], core_send.at[t, j], core_recv.at[t, j], core
        )

    def start(copies):
        for copy in copies:
            copy.start()

    def fill(i, carry):
        half, piece = i // tiles, lax.rem(i, tiles)

        @pl.when(i == 1)
        def _():
            pl.semaphore_wait(barrier, group - 1 + n_region - 1)
            start([phase_copy()])
            start([omega_piece(j) for j in range(tiles)])
            coarse_ref[0, 0, row] = state_ref[0].astype(BF16)
            start(near_copies(0))
            start(far_copies(0))

        @pl.when(i == tiles)
        def _():
            phase_copy().wait_recv()

        @pl.when(i >= tiles)
        def _():
            omega_piece(piece).wait_recv()

        down = pl.multiple_of(piece * tile, tile)
        part = (omega_ref[half, :, pl.ds(down, tile)].astype(F32) * INV_TURN).T
        high = part.astype(BF16)
        low = (part - high.astype(F32)).astype(BF16)
        column = column_of(phase_ref[half, :, pl.ds(down, tile)] * INV_TURN)
        both = jnp.concatenate([high, low], axis=1)
        value = feature_tile(both, column, samples_ref[...])
        feat_ref[half, pl.ds(down, tile), :] = value
        flip_ref[half, :, pl.ds(down, tile)] = value.T
        return carry

    rho = jnp.full((1, 128), penalty_ref[0], F32)
    history = jnp.zeros((1, 128), F32)
    lane = lax.broadcasted_iota(jnp.int32, (1, 128), 1)
    with jax.named_scope("load0"):
        for load in loads[:6]:
            load.wait()
        for load in loads[6:]:
            load.start()
        samples_ref[:, inputs:] = samples_ref[:, :inputs]
    with jax.named_scope("fill"):
        lax.fori_loop(0, 2 * tiles, fill, 0)
    weights, duals, consensus = state_ref[0], state_ref[1], state_ref[2]

    for t in range(ITERS):
        with jax.named_scope("near_wait"):
            arrived(coarse_ref.at[t, 0, pl.ds(0, n_row - 1)], crow_recv.at[t])
        if t == 0:
            loads[6].wait()
            loads[7].wait()
        with jax.named_scope("pred_near"):
            near = coarse_ref[t, 0].reshape(outputs, width)
            for j in range(chunks):
                span = slice(j * chunk, (j + 1) * chunk)
                acc_ref[:, span] = dot(near, feat_ref[0, :, span])
        with jax.named_scope("far_wait"):
            arrived(coarse_ref.at[t, 1], cside_recv.at[t])
        with jax.named_scope("pred_far"):
            far = coarse_ref[t, 1].reshape(outputs, width)
            for j in range(chunks):
                if t > 0 and j == chunks - 1:
                    with jax.named_scope("share_mean"):
                        share_mean(t - 1)
                span = slice(j * chunk, (j + 1) * chunk)
                part = gain * (acc_ref[:, span] + dot(far, feat_ref[1, :, span]))
                acc_ref[:, span] = part
                part_ref[t, j] = part.astype(BF16)
                core_copy(t, j).start()
        with jax.named_scope("resid"):
            for j in range(chunks):
                span = slice(j * chunk, (j + 1) * chunk)
                core_copy(t, j).wait_recv()
                predicted = acc_ref[:, span] + other_ref[t, j].astype(F32)
                gap_value = predicted - targets_ref[:, span].astype(F32)
                resid_ref[:, span] = (member_ref[:, span].astype(F32) * gap_value).astype(BF16)

        with jax.named_scope("grad_far"):
            for p in range(PARTS):
                span = slice(p * piece_width, (p + 1) * piece_width)
                value = dot(resid_ref[...], flip_ref[1, :, span])
                gfar_ref[t, p] = value.astype(BF16).reshape(n_row, narrow, piece_width)
                for k in range(n_row):
                    target = lax.rem(row + k, n_row)
                    copy = remote(
                        gfar_ref.at[t, p, target], gside_ref.at[t, p, k], gside_send.at[t],
                        gside_recv.at[t], far_peer(k),
                    )
                    copy.start()
        with jax.named_scope("grad_near"):
            for p in range(PARTS):
                span = slice(p * piece_width, (p + 1) * piece_width)
                value = dot(resid_ref[...], flip_ref[0, :, span])
                value = value.reshape(n_row, narrow, piece_width)
                gown_ref[p] = value
                gsend_ref[t, p] = value.astype(BF16)
                for k in range(1, n_row):
                    target = lax.rem(row + k, n_row)
                    copy = remote(
                        gsend_ref.at[t, p, target], grow_ref.at[t, p, k], grow_send.at[t],
                        grow_recv.at[t], row_peer(k),
                    )
                    copy.start()
        if t == 0:
            with jax.named_scope("invert"):
                loads[8].wait()
                invert(min(256, width), factor_ref, dinv_ref, strict_ref, solve_ref)
        else:
            with jax.named_scope("finish_region"):
                apart, duals, consensus = finish_region(t - 1)
        dinv = dinv_ref[...]
        with jax.named_scope("grad_wait"):
            arrived(gside_ref.at[t], gside_recv.at[t])
            arrived(grow_ref.at[t, :, pl.ds(1, n_row - 1)], grow_recv.at[t])
            gradient = []
            for p in range(PARTS):
                value = gown_ref[p, row]
                for k in range(n_row):
                    value = value + gside_ref[t, p, k].astype(F32)
                for k in range(1, n_row):
                    value = value + grow_ref[t, p, k].astype(F32)
                gradient.append(value)
            gradient = gain * jnp.concatenate(gradient, axis=1)
        with jax.named_scope("solve"):
            scalar = rho[:, :1]
            if t == 0:
                right = gradient + scalar * (weights - consensus + duals)
            else:
                right = jnp.concatenate([gradient + scalar * duals, apart], axis=0)
            forward = right * dinv
            forward = forward + dot_nt(forward.astype(BF16), solve_ref[...])
            update = (forward + dot(forward.astype(BF16), solve_ref[...])) * dinv
        if t > 0:
            with jax.named_scope("finish_gap"):
                rho, duals, history = finish_gap(t - 1, rho, duals, history)
            scalar = rho[:, :1]
            update = update[:narrow] + scalar * update[narrow:]
        weights = weights - update
        if t < ITERS - 1:
            coarse_ref[t + 1, 0, row] = weights.astype(BF16)
            start(near_copies(t + 1))

        total = scalar * (weights + duals)
        for c in range(n_region):
            down, right = 8 * (c // lanes), 128 * (c % lanes)
            rs_send_ref[t, c, :8] = total[down : down + 8, right : right + 128]
            rs_send_ref[t, c, 8:] = jnp.broadcast_to(scalar, (8, 128))
        rs_recv_ref[t, region] = rs_send_ref[t, region]
        for k in range(1, n_region):
            owner = lax.rem(region + k, n_region)
            copy = remote(
                rs_send_ref.at[t, owner, pl.ds(0, 9)], rs_recv_ref.at[t, region, pl.ds(0, 9)],
                rs_send.at[t], rs_recv.at[t], region_peer(k),
            )
            copy.start()
        if t < ITERS - 1:
            start(far_copies(t + 1))

        def share_mean(s):
            arrived(rs_recv_ref.at[s, pl.ds(0, n_region - 1), pl.ds(0, 9)], rs_recv.at[s])
            total = rs_recv_ref[s, 0, :9]
            for r in range(1, n_region):
                total = total + rs_recv_ref[s, r, :9]
            mean_ref[s, region] = total[:8] / total[8:9]
            mine = mean_ref.at[s, region]
            for k in range(1, n_region):
                remote(mine, mine, mean_send.at[s], mean_recv.at[s], region_peer(k)).start()

        def finish_region(s, weights=weights, duals=duals, consensus=consensus):
            arrived(mean_ref.at[s, pl.ds(0, n_region - 1)], mean_recv.at[s])
            updated = jnp.concatenate(
                [
                    jnp.concatenate([mean_ref[s, h * lanes + j] for j in range(lanes)], axis=1)
                    for h in range(narrow // 8)
                ],
                axis=0,
            )
            gap = jnp.sum(jnp.square(weights - updated), keepdims=True).reshape(1, 1)
            drift = jnp.sum(jnp.square(updated - consensus), keepdims=True).reshape(1, 1)
            level = lax.broadcasted_iota(jnp.int32, (8, 128), 0)
            gap_ref[s, place] = jnp.where(level == 0, gap, drift)
            mine = gap_ref.at[s, place]
            for k in range(1, group):
                remote(mine, mine, gap_send.at[s], gap_recv.at[s], group_peer(k)).start()
            return weights - updated, duals + weights - updated, updated

        def finish_gap(s, rho, duals, history):
            arrived(gap_ref.at[s, pl.ds(0, group - 1)], gap_recv.at[s])
            total = jnp.sum(gap_ref[s], axis=0)
            gap, drift = total[0:1], total[1:2]
            drift = rho * rho * drift
            renewed = rho * jnp.sqrt((gap + offset) / (drift + offset))
            duals = duals * (rho / renewed)[:, :1]
            return renewed, duals, jnp.where(lane == s, renewed, history)

    def store(rows, value):
        state_ref[rows] = value
        copy = pltpu.make_async_copy(state_ref.at[rows], out_hbm.at[rows], store_sem.at[rows])
        copy.start()
        return copy

    stores = [store(0, weights)]
    with jax.named_scope("last_mean"):
        share_mean(ITERS - 1)
    with jax.named_scope("last_region"):
        apart, duals, consensus = finish_region(ITERS - 1)
    stores.append(store(2, consensus))
    with jax.named_scope("last_gap"):
        rho, duals, history = finish_gap(ITERS - 1, rho, duals, history)
    stores.append(store(1, duals))
    stores.append(store(3, jnp.broadcast_to(jnp.tile(history, (1, width // 128)), (narrow, width))))
    with jax.named_scope("drain"):
        phase_copy().wait_send()
        for i in range(tiles):
            omega_piece(i).wait_send()
        for t in range(ITERS):
            sent(coarse_ref.at[t, 0, pl.ds(0, n_row - 1)], crow_send.at[t])
            sent(coarse_ref.at[t, 1], cside_send.at[t])
            for j in range(chunks):
                core_copy(t, j).wait_send()
            sent(gside_ref.at[t], gside_send.at[t])
            sent(grow_ref.at[t, :, pl.ds(1, n_row - 1)], grow_send.at[t])
            sent(rs_recv_ref.at[t, pl.ds(0, n_region - 1), pl.ds(0, 9)], rs_send.at[t])
            sent(mean_ref.at[t, pl.ds(0, n_region - 1)], mean_send.at[t])
            sent(gap_ref.at[t, pl.ds(0, group - 1)], gap_send.at[t])
        for copy in stores:
            copy.wait()


def admm(sizes, offset, scale, penalty, samples, targets, member, omega, phase, factors, *state):
    n_region, n_feat, n_row = sizes
    narrow, width = state[0].shape
    outputs = n_row * narrow
    inputs = omega.shape[0]
    count = samples.shape[0] // (n_feat // CORES)
    chunk = min(CHUNK, count)
    chunks = count // chunk
    group = n_feat * n_row
    part = (n_row, narrow, width // PARTS)
    tiles = width // min(512, width // PARTS)
    hbm = pl.BlockSpec(memory_space=pl.ANY)
    dma = pltpu.SemaphoreType.DMA
    return pl.pallas_call(
        functools.partial(admm_kernel, sizes, offset, scale),
        in_specs=[pl.BlockSpec(memory_space=pltpu.SMEM)] + [hbm] * 9,
        out_specs=hbm,
        out_shape=jax.ShapeDtypeStruct((4, narrow, width), F32),
        scratch_shapes=[
            pltpu.VMEM((width, width), F32),
            pltpu.VMEM((1, width), F32),
            pltpu.VMEM((width, width), BF16),
            pltpu.VMEM((width, width), BF16),
            pltpu.VMEM((count, 2 * inputs), BF16),
            pltpu.VMEM((outputs, count), BF16),
            pltpu.VMEM((1, count), jnp.int32),
            pltpu.VMEM((2, inputs, width), BF16),
            pltpu.VMEM((2, 1, width), F32),
            pltpu.VMEM((4, narrow, width), F32),
            pltpu.VMEM((2, width, count), BF16),
            pltpu.VMEM((2, count, width), BF16),
            pltpu.VMEM((ITERS, 2, n_row, narrow, width), BF16),
            pltpu.VMEM((outputs, count), F32),
            pltpu.VMEM((ITERS, chunks, outputs, chunk), BF16),
            pltpu.VMEM((ITERS, chunks, outputs, chunk), BF16),
            pltpu.VMEM((outputs, count), BF16),
            pltpu.VMEM((ITERS, PARTS) + part, BF16),
            pltpu.VMEM((ITERS, PARTS) + part, BF16),
            pltpu.VMEM((PARTS,) + part, F32),
            pltpu.VMEM((ITERS, PARTS) + part, BF16),
            pltpu.VMEM((ITERS, PARTS) + part, BF16),
            pltpu.VMEM((ITERS, n_region, 16, 128), F32),
            pltpu.VMEM((ITERS, n_region, 16, 128), F32),
            pltpu.VMEM((ITERS, n_region, 8, 128), F32),
            pltpu.VMEM((ITERS, group, 8, 128), F32),
            dma((9,)),
            dma((4,)),
            dma((tiles,)),
            dma((tiles,)),
            dma((1,)),
            dma((1,)),
            dma((ITERS,)),
            dma((ITERS,)),
            dma((ITERS,)),
            dma((ITERS,)),
            dma((ITERS, chunks)),
            dma((ITERS, chunks)),
            dma((ITERS,)),
            dma((ITERS,)),
            dma((ITERS,)),
            dma((ITERS,)),
            dma((ITERS,)),
            dma((ITERS,)),
            dma((ITERS,)),
            dma((ITERS,)),
            dma((ITERS,)),
            dma((ITERS,)),
        ],
        compiler_params=pltpu.CompilerParams(
            collective_id=0, has_side_effects=True, vmem_limit_bytes=63 * 2**20
        ),
        name="admm",
    )(penalty, samples, targets, member, omega, phase, factors, *state)


def per_device(
    sizes,
    samples,
    targets,
    member,
    omega,
    phase,
    factors,
    weights_init,
    duals_init,
    consensus_init,
    penalty_init,
):
    n_region, n_feat, n_row = sizes
    total_features = n_feat * omega.shape[1]
    total_outputs = targets.shape[1]
    offset = 0.01 * total_features * total_outputs
    scale = math.sqrt(2.0 / total_features)
    final = admm(
        sizes, offset, scale, penalty_init, samples, targets.T, member[None, :], omega,
        phase[None, :], factors, weights_init.T, duals_init.T, consensus_init.T,
    )
    return (final[0].T, final[1].T, final[2].T, final[3, :1, :ITERS])


def solution(mesh):
    sizes = (mesh.shape["region"], mesh.shape["feat"], mesh.shape["row"])
    return jax.shard_map(
        functools.partial(per_device, sizes),
        mesh=mesh,
        in_specs=(
            P(("region", "row"), None),
            P(("region", "row"), None),
            P(("region", "row")),
            P(None, "feat"),
            P("feat"),
            P(("region", "feat"), None),
            P(("region", "feat"), "row"),
            P(("region", "feat"), "row"),
            P("feat", "row"),
            P("region"),
        ),
        out_specs=(
            P(("region", "feat"), "row"),
            P(("region", "feat"), "row"),
            P("feat", "row"),
            P("region", None),
        ),
        check_vma=False,
    )
```

time: 120 us -> 95.5 us (0.80)
  Pallas kernels: 116 us -> 91.3 us
    pallas_call x1, Pallas kernels: 116 us -> 91.3 us  [admm(): pl.pallas_call(functools.partial(admm_kernel, sizes, offset, scale), in_s...]
where the time goes in v2:
time: 95.5 us; the launch traced here: 95.3 us
  Pallas kernels  91.3 us (96%)
  local copies, waits for them, and re-layouts  2.76 us (3%)
  between operations  1.29 us (1%)
    pallas_call x1, Pallas kernels, admm(): pl.pallas_call(functools.partial(admm_kernel, sizes, offset, scale), in_s...  91.3 us

profile of v2, /device:TPU:1, one launch (start us, length us, event | category | flops | bytes accessed | tf_op | source)
XLA Modules:
  0.0 95.3 jit_solution(17445957221452776772)
XLA Ops:
  1.3 91.3 %admm.1 = f32[4,16,1024]{2,1,0:T(8,128)} custom-call(f32[1]{0:T(128)S(6)} %copy.14.penalty_ref, bf16[8192,128]{1,0:T(8,128)(2,1)} %samples_hbm.1, bf16[64,8192]{1,0:T(8,128)(2,1)} %bitcast.20, s32[1,8192]{1,0:T(1,128)} %bitcast.24, bf16[128,1024]{1,0:T(8,128)(2,1)} %omega_hbm.1, f32[1,1024]{1,0:T(1,128)} %bitcast.25, f32[1024,1024]{1,0:T(8,128)} %factor_hbm.1, ...), custom_call_target="tpu_custom_call" | custom-call | tf_op jit(solution)/shard_map/admm/pallas_call | solution.py:491
  92.6 1.6 %slice_bitcast_fusion = (f32[1024,16]{0,1:T(8,128)}, f32[1024,16]{0,1:T(8,128)}, f32[1024,16]{0,1:T(8,128)}) fusion(f32[4,16,1024]{2,1,0:T(8,128)} %admm.1), kind=kLoop, calls=%fused_computation | loop fusion | bytes 393216 | tf_op jit(solution)/shard_map/transpose | solution.py:575
  94.1 1.2 %slice_bitcast_fusion.3 = f32[1,3]{1,0:T(1,128)} fusion(f32[4,16,1024]{2,1,0:T(8,128)} %admm.1), kind=kLoop, calls=%fused_computation.3 | loop fusion | bytes 24 | tf_op jit(solution)/shard_map/squeeze | solution.py:575

commit v3 on v2

--- a/solution.py
+++ b/solution.py
@@ -76,11 +76,25 @@
         width *= 2
 
 
+def lower(rows, t_ref):
+    size = t_ref.shape[0]
+    step = min(256, size)
+    pieces = [dot_nt(rows[:, : i + step], t_ref[i : i + step, : i + step]) for i in range(0, size, step)]
+    return jnp.concatenate(pieces, axis=1)
+
+
+def lower_flipped(rows, t_ref):
+    size = t_ref.shape[0]
+    step = min(256, size)
+    pieces = [dot(rows[:, i:], t_ref[i:, i : i + step]) for i in range(0, size, step)]
+    return jnp.concatenate(pieces, axis=1)
+
+
 def admm_kernel(
     sizes,
     offset,
     scale,
-    penalty_ref,
+    penalty_hbm,
     samples_hbm,
     targets_hbm,
     member_hbm,
@@ -101,6 +115,7 @@
     omega_ref,
     phase_ref,
     state_ref,
+    penalty_ref,
     feat_ref,
     flip_ref,
     coarse_ref,
@@ -151,7 +166,8 @@
     chunks = count // chunk
     piece_width = width // PARTS
     tile = min(512, piece_width)
-    tiles = width // tile
+    small = tile // 2
+    ratio, tiles, pieces = tile // small, width // tile, width // small
     region, feat, row = lax.axis_index("region"), lax.axis_index("feat"), lax.axis_index("row")
     group = n_feat * n_row
     place = feat * n_row + row
@@ -186,11 +202,12 @@
         pltpu.make_async_copy(weights_hbm, state_ref.at[0], load_sem.at[3]),
         pltpu.make_async_copy(duals_hbm, state_ref.at[1], load_sem.at[4]),
         pltpu.make_async_copy(consensus_hbm, state_ref.at[2], load_sem.at[5]),
+        pltpu.make_async_copy(penalty_hbm, penalty_ref, load_sem.at[9]),
         pltpu.make_async_copy(targets_hbm.at[:, span], targets_ref, load_sem.at[6]),
         pltpu.make_async_copy(member_hbm.at[:, span], member_ref, load_sem.at[7]),
         pltpu.make_async_copy(factor_hbm, factor_ref, load_sem.at[8]),
     ]
-    for load in loads[:6]:
+    for load in loads[:7]:
         load.start()
 
     barrier = pltpu.get_barrier_semaphore()
@@ -201,7 +218,7 @@
 
     def column_of(line):
         pieces = []
-        for j in range(tile // 128):
+        for j in range(line.shape[1] // 128):
             level = lax.broadcasted_iota(jnp.int32, (128, 128), 0)
             across = lax.broadcasted_iota(jnp.int32, (128, 128), 1)
             only = jnp.where(level == across, line[:, 128 * j : 128 * (j + 1)], 0.0)
@@ -209,7 +226,7 @@
         return jnp.concatenate(pieces, axis=0)
 
     def omega_piece(i):
-        span = pl.ds(pl.multiple_of(i * tile, tile), tile)
+        span = pl.ds(pl.multiple_of(i * small, small), small)
         return remote(
             omega_ref.at[0, :, span], omega_ref.at[1, :, span], omega_send.at[i], omega_recv.at[i],
             side,
@@ -247,14 +264,28 @@
         for copy in copies:
             copy.start()
 
-    def fill(i, carry):
-        half, piece = i // tiles, lax.rem(i, tiles)
-
+    def fill(half, down, size):
+        rows = pl.ds(pl.multiple_of(down, size), size)
+        part = (omega_ref[half, :, rows].astype(F32) * INV_TURN).T
+        high = part.astype(BF16)
+        low = (part - high.astype(F32)).astype(BF16)
+        column = column_of(phase_ref[half, :, rows] * INV_TURN)
+        both = jnp.concatenate([high, low], axis=1)
+        value = feature_tile(both, column, samples_ref[...])
+        feat_ref[half, rows, :] = value
+        flip_ref[half, :, rows] = value.T
+
+    def fill_small(i, carry):
+        omega_piece(i).wait_recv()
+        fill(1, i * small, small)
+        return carry
+
+    def fill_large(i, carry):
         @pl.when(i == 1)
         def _():
             pl.semaphore_wait(barrier, group - 1 + n_region - 1)
             start([phase_copy()])
-            start([omega_piece(j) for j in range(tiles)])
+            start([omega_piece(j) for j in range(pieces)])
             coarse_ref[0, 0, row] = state_ref[0].astype(BF16)
             start(near_copies(0))
             start(far_copies(0))
@@ -262,41 +293,36 @@
         @pl.when(i == tiles)
         def _():
             phase_copy().wait_recv()
+            lax.fori_loop(0, ratio, fill_small, 0)
 
         @pl.when(i >= tiles)
         def _():
-            omega_piece(piece).wait_recv()
-
-        down = pl.multiple_of(piece * tile, tile)
-        part = (omega_ref[half, :, pl.ds(down, tile)].astype(F32) * INV_TURN).T
-        high = part.astype(BF16)
-        low = (part - high.astype(F32)).astype(BF16)
-        column = column_of(phase_ref[half, :, pl.ds(down, tile)] * INV_TURN)
-        both = jnp.concatenate([high, low], axis=1)
-        value = feature_tile(both, column, samples_ref[...])
-        feat_ref[half, pl.ds(down, tile), :] = value
-        flip_ref[half, :, pl.ds(down, tile)] = value.T
+            for j in range(ratio):
+                omega_piece(ratio * lax.rem(i + 1, tiles) + j).wait_recv()
+
+        half = i // tiles
+        fill(half, (i - half * (tiles - 1)) * tile, tile)
         return carry
 
-    rho = jnp.full((1, 128), penalty_ref[0], F32)
     history = jnp.zeros((1, 128), F32)
     lane = lax.broadcasted_iota(jnp.int32, (1, 128), 1)
     with jax.named_scope("load0"):
-        for load in loads[:6]:
+        for load in loads[:7]:
             load.wait()
-        for load in loads[6:]:
+        for load in loads[7:]:
             load.start()
         samples_ref[:, inputs:] = samples_ref[:, :inputs]
     with jax.named_scope("fill"):
-        lax.fori_loop(0, 2 * tiles, fill, 0)
+        lax.fori_loop(0, 2 * tiles - 1, fill_large, 0)
     weights, duals, consensus = state_ref[0], state_ref[1], state_ref[2]
+    rho = jnp.broadcast_to(penalty_ref[...], (1, 128))
 
     for t in range(ITERS):
         with jax.named_scope("near_wait"):
             arrived(coarse_ref.at[t, 0, pl.ds(0, n_row - 1)], crow_recv.at[t])
         if t == 0:
-            loads[6].wait()
             loads[7].wait()
+            loads[8].wait()
         with jax.named_scope("pred_near"):
             near = coarse_ref[t, 0].reshape(outputs, width)
             for j in range(chunks):
@@ -351,7 +377,7 @@
                     copy.start()
         if t == 0:
             with jax.named_scope("invert"):
-                loads[8].wait()
+                loads[9].wait()
                 invert(min(256, width), factor_ref, dinv_ref, strict_ref, solve_ref)
         else:
             with jax.named_scope("finish_region"):
@@ -376,8 +402,8 @@
             else:
                 right = jnp.concatenate([gradient + scalar * duals, apart], axis=0)
             forward = right * dinv
-            forward = forward + dot_nt(forward.astype(BF16), solve_ref[...])
-            update = (forward + dot(forward.astype(BF16), solve_ref[...])) * dinv
+            forward = forward + lower(forward.astype(BF16), solve_ref)
+            update = (forward + lower_flipped(forward.astype(BF16), solve_ref)) * dinv
         if t > 0:
             with jax.named_scope("finish_gap"):
                 rho, duals, history = finish_gap(t - 1, rho, duals, history)
@@ -425,17 +451,17 @@
             )
             gap = jnp.sum(jnp.square(weights - updated), keepdims=True).reshape(1, 1)
             drift = jnp.sum(jnp.square(updated - consensus), keepdims=True).reshape(1, 1)
-            level = lax.broadcasted_iota(jnp.int32, (8, 128), 0)
-            gap_ref[s, place] = jnp.where(level == 0, gap, drift)
-            mine = gap_ref.at[s, place]
+            gap_ref[s, place, :1] = jnp.where(lane < 64, gap, drift)
+            mine = gap_ref.at[s, place, pl.ds(0, 1)]
             for k in range(1, group):
                 remote(mine, mine, gap_send.at[s], gap_recv.at[s], group_peer(k)).start()
             return weights - updated, duals + weights - updated, updated
 
         def finish_gap(s, rho, duals, history):
-            arrived(gap_ref.at[s, pl.ds(0, group - 1)], gap_recv.at[s])
-            total = jnp.sum(gap_ref[s], axis=0)
-            gap, drift = total[0:1], total[1:2]
+            arrived(gap_ref.at[s, pl.ds(0, group - 1), pl.ds(0, 1)], gap_recv.at[s])
+            total = jnp.sum(gap_ref[s, :, :1], axis=0)
+            gap = jnp.broadcast_to(total[:, :1], (1, 128))
+            drift = jnp.broadcast_to(total[:, 64:65], (1, 128))
             drift = rho * rho * drift
             renewed = rho * jnp.sqrt((gap + offset) / (drift + offset))
             duals = duals * (rho / renewed)[:, :1]
@@ -448,6 +474,21 @@
         return copy
 
     stores = [store(0, weights)]
+    with jax.named_scope("drain_early"):
+        phase_copy().wait_send()
+        for i in range(pieces):
+            omega_piece(i).wait_send()
+        for t in range(ITERS):
+            sent(coarse_ref.at[t, 0, pl.ds(0, n_row - 1)], crow_send.at[t])
+            sent(coarse_ref.at[t, 1], cside_send.at[t])
+            for j in range(chunks):
+                core_copy(t, j).wait_send()
+            sent(gside_ref.at[t], gside_send.at[t])
+            sent(grow_ref.at[t, :, pl.ds(1, n_row - 1)], grow_send.at[t])
+            sent(rs_recv_ref.at[t, pl.ds(0, n_region - 1), pl.ds(0, 9)], rs_send.at[t])
+            if t < ITERS - 1:
+                sent(mean_ref.at[t, pl.ds(0, n_region - 1)], mean_send.at[t])
+                sent(gap_ref.at[t, pl.ds(0, group - 1), pl.ds(0, 1)], gap_send.at[t])
     with jax.named_scope("last_mean"):
         share_mean(ITERS - 1)
     with jax.named_scope("last_region"):
@@ -458,19 +499,8 @@
     stores.append(store(1, duals))
     stores.append(store(3, jnp.broadcast_to(jnp.tile(history, (1, width // 128)), (narrow, width))))
     with jax.named_scope("drain"):
-        phase_copy().wait_send()
-        for i in range(tiles):
-            omega_piece(i).wait_send()
-        for t in range(ITERS):
-            sent(coarse_ref.at[t, 0, pl.ds(0, n_row - 1)], crow_send.at[t])
-            sent(coarse_ref.at[t, 1], cside_send.at[t])
-            for j in range(chunks):
-                core_copy(t, j).wait_send()
-            sent(gside_ref.at[t], gside_send.at[t])
-            sent(grow_ref.at[t, :, pl.ds(1, n_row - 1)], grow_send.at[t])
-            sent(rs_recv_ref.at[t, pl.ds(0, n_region - 1), pl.ds(0, 9)], rs_send.at[t])
-            sent(mean_ref.at[t, pl.ds(0, n_region - 1)], mean_send.at[t])
-            sent(gap_ref.at[t, pl.ds(0, group - 1)], gap_send.at[t])
+        sent(mean_ref.at[ITERS - 1, pl.ds(0, n_region - 1)], mean_send.at[ITERS - 1])
+        sent(gap_ref.at[ITERS - 1, pl.ds(0, group - 1), pl.ds(0, 1)], gap_send.at[ITERS - 1])
         for copy in stores:
             copy.wait()
 
@@ -490,7 +520,7 @@
     dma = pltpu.SemaphoreType.DMA
     return pl.pallas_call(
         functools.partial(admm_kernel, sizes, offset, scale),
-        in_specs=[pl.BlockSpec(memory_space=pltpu.SMEM)] + [hbm] * 9,
+        in_specs=[hbm] * 10,
         out_specs=hbm,
         out_shape=jax.ShapeDtypeStruct((4, narrow, width), F32),
         scratch_shapes=[
@@ -504,6 +534,7 @@
             pltpu.VMEM((2, inputs, width), BF16),
             pltpu.VMEM((2, 1, width), F32),
             pltpu.VMEM((4, narrow, width), F32),
+            pltpu.VMEM((1, 1), F32),
             pltpu.VMEM((2, width, count), BF16),
             pltpu.VMEM((2, count, width), BF16),
             pltpu.VMEM((ITERS, 2, n_row, narrow, width), BF16),
@@ -520,10 +551,10 @@
             pltpu.VMEM((ITERS, n_region, 16, 128), F32),
             pltpu.VMEM((ITERS, n_region, 8, 128), F32),
             pltpu.VMEM((ITERS, group, 8, 128), F32),
-            dma((9,)),
+            dma((10,)),
             dma((4,)),
-            dma((tiles,)),
-            dma((tiles,)),
+            dma((2 * tiles,)),
+            dma((2 * tiles,)),
             dma((1,)),
             dma((1,)),
             dma((ITERS,)),
@@ -569,7 +600,7 @@
     offset = 0.01 * total_features * total_outputs
     scale = math.sqrt(2.0 / total_features)
     final = admm(
-        sizes, offset, scale, penalty_init, samples, targets.T, member[None, :], omega,
+        sizes, offset, scale, penalty_init[None, :], samples, targets.T, member[None, :], omega,
         phase[None, :], factors, weights_init.T, duals_init.T, consensus_init.T,
     )
     return (final[0].T, final[1].T, final[2].T, final[3, :1, :ITERS])

time: 95.5 us -> 94.2 us (0.986)
  Pallas kernels: 91.3 us -> 89.9 us
    pallas_call x1, Pallas kernels: 91.3 us -> 89.9 us  [admm(): pl.pallas_call(functools.partial(admm_kernel, sizes, offset, scale), in_s...]
where the time goes in v3:
time: 94.2 us; the launch traced here: 94 us
  Pallas kernels  89.9 us (95%)
  local copies, waits for them, and re-layouts  2.76 us (3%)
  between operations  1.29 us (1%)
    pallas_call x1, Pallas kernels, admm(): pl.pallas_call(functools.partial(admm_kernel, sizes, offset, scale), in_s...  89.9 us

profile of v3, /device:TPU:1, one launch (start us, length us, event | category | flops | bytes accessed | tf_op | source)
XLA Modules:
  0.0 94.0 jit_solution(7545064062950587874)
XLA Ops:
  1.3 89.9 %admm.1 = f32[4,16,1024]{2,1,0:T(8,128)} custom-call(f32[1,1]{1,0:T(1,128)} %bitcast.21.penalty_hbm, bf16[8192,128]{1,0:T(8,128)(2,1)} %samples_hbm.1, bf16[64,8192]{1,0:T(8,128)(2,1)} %bitcast.22, s32[1,8192]{1,0:T(1,128)} %bitcast.26, bf16[128,1024]{1,0:T(8,128)(2,1)} %omega_hbm.1, f32[1,1024]{1,0:T(1,128)} %bitcast.27, f32[1024,1024]{1,0:T(8,128)} %factor_hbm.1, ...), custom_call_target="tpu_custom_call" | custom-call | tf_op jit(solution)/shard_map/admm/pallas_call | solution.py:521
  91.2 1.6 %slice_bitcast_fusion = (f32[1024,16]{0,1:T(8,128)}, f32[1024,16]{0,1:T(8,128)}, f32[1024,16]{0,1:T(8,128)}) fusion(f32[4,16,1024]{2,1,0:T(8,128)} %admm.1), kind=kLoop, calls=%fused_computation | loop fusion | bytes 393216 | tf_op jit(solution)/shard_map/transpose | solution.py:606
  92.8 1.2 %slice_bitcast_fusion.3 = f32[1,3]{1,0:T(1,128)} fusion(f32[4,16,1024]{2,1,0:T(8,128)} %admm.1), kind=kLoop, calls=%fused_computation.3 | loop fusion | bytes 24 | tf_op jit(solution)/shard_map/squeeze | solution.py:606

commit v4 on v3

--- a/solution.py
+++ b/solution.py
@@ -174,6 +174,20 @@
     side = (region, lax.rem(feat + CORES, n_feat), row)
     core = (region, feat + 1 - 2 * lax.rem(feat, CORES), row)
 
+    def apart_rows(k):
+        return min(k % n_row, n_row - k % n_row)
+
+    def apart_regions(k):
+        return min(k // CORES, n_region // CORES - k // CORES) + 2 * (k % CORES)
+
+    def apart_group(k):
+        return apart_rows(k) + 0.5 * min(k // n_row, n_feat - k // n_row)
+
+    near_order = sorted(range(1, n_row), key=apart_rows, reverse=True)
+    far_order = sorted(range(n_row), key=apart_rows, reverse=True)
+    region_order = sorted(range(1, n_region), key=apart_regions, reverse=True)
+    group_order = sorted(range(1, group), key=apart_group, reverse=True)
+
     def row_peer(k):
         return (region, feat, lax.rem(row + k, n_row))
 
@@ -211,9 +225,9 @@
         load.start()
 
     barrier = pltpu.get_barrier_semaphore()
-    for k in range(1, group):
+    for k in group_order:
         pl.semaphore_signal(barrier, inc=1, device_id=group_peer(k), device_id_type=MESH)
-    for k in range(1, n_region):
+    for k in region_order:
         pl.semaphore_signal(barrier, inc=1, device_id=region_peer(k), device_id_type=MESH)
 
     def column_of(line):
@@ -239,14 +253,14 @@
         mine = coarse_ref.at[t, 0, row]
         return [
             remote(mine, mine, crow_send.at[t], crow_recv.at[t], row_peer(k))
-            for k in range(1, n_row)
+            for k in near_order
         ]
 
     def far_copies(t):
         mine, there = coarse_ref.at[t, 0, row], coarse_ref.at[t, 1, row]
         return [
             remote(mine, there, cside_send.at[t], cside_recv.at[t], far_peer(k))
-            for k in range(n_row)
+            for k in far_order
         ]
 
     def arrived(pieces, semaphore):
@@ -328,14 +342,14 @@
             for j in range(chunks):
                 span = slice(j * chunk, (j + 1) * chunk)
                 acc_ref[:, span] = dot(near, feat_ref[0, :, span])
+        if t > 0:
+            with jax.named_scope("share_mean"):
+                share_mean(t - 1)
         with jax.named_scope("far_wait"):
             arrived(coarse_ref.at[t, 1], cside_recv.at[t])
         with jax.named_scope("pred_far"):
             far = coarse_ref[t, 1].reshape(outputs, width)
             for j in range(chunks):
-                if t > 0 and j == chunks - 1:
-                    with jax.named_scope("share_mean"):
-                        share_mean(t - 1)
                 span = slice(j * chunk, (j + 1) * chunk)
                 part = gain * (acc_ref[:, span] + dot(far, feat_ref[1, :, span]))
                 acc_ref[:, span] = part
@@ -354,7 +368,7 @@
                 span = slice(p * piece_width, (p + 1) * piece_width)
                 value = dot(resid_ref[...], flip_ref[1, :, span])
                 gfar_ref[t, p] = value.astype(BF16).reshape(n_row, narrow, piece_width)
-                for k in range(n_row):
+                for k in far_order:
                     target = lax.rem(row + k, n_row)
                     copy = remote(
                         gfar_ref.at[t, p, target], gside_ref.at[t, p, k], gside_send.at[t],
@@ -368,7 +382,7 @@
                 value = value.reshape(n_row, narrow, piece_width)
                 gown_ref[p] = value
                 gsend_ref[t, p] = value.astype(BF16)
-                for k in range(1, n_row):
+                for k in near_order:
                     target = lax.rem(row + k, n_row)
                     copy = remote(
                         gsend_ref.at[t, p, target], grow_ref.at[t, p, k], grow_send.at[t],
@@ -420,7 +434,7 @@
             rs_send_ref[t, c, :8] = total[down : down + 8, right : right + 128]
             rs_send_ref[t, c, 8:] = jnp.broadcast_to(scalar, (8, 128))
         rs_recv_ref[t, region] = rs_send_ref[t, region]
-        for k in range(1, n_region):
+        for k in region_order:
             owner = lax.rem(region + k, n_region)
             copy = remote(
                 rs_send_ref.at[t, owner, pl.ds(0, 9)], rs_recv_ref.at[t, region, pl.ds(0, 9)],
@@ -437,7 +451,7 @@
                 total = total + rs_recv_ref[s, r, :9]
             mean_ref[s, region] = total[:8] / total[8:9]
             mine = mean_ref.at[s, region]
-            for k in range(1, n_region):
+            for k in region_order:
                 remote(mine, mine, mean_send.at[s], mean_recv.at[s], region_peer(k)).start()
 
         def finish_region(s, weights=weights, duals=duals, consensus=consensus):
@@ -453,7 +467,7 @@
             drift = jnp.sum(jnp.square(updated - consensus), keepdims=True).reshape(1, 1)
             gap_ref[s, place, :1] = jnp.where(lane < 64, gap, drift)
             mine = gap_ref.at[s, place, pl.ds(0, 1)]
-            for k in range(1, group):
+            for k in group_order:
                 remote(mine, mine, gap_send.at[s], gap_recv.at[s], group_peer(k)).start()
             return weights - updated, duals + weights - updated, updated
 

time: 94.2 us -> 91.2 us (0.968)
  Pallas kernels: 89.9 us -> 87 us
    pallas_call x1, Pallas kernels: 89.9 us -> 87 us  [admm(): pl.pallas_call(functools.partial(admm_kernel, sizes, offset, scale), in_s...]
where the time goes in v4:
time: 91.2 us; the launch traced here: 91 us
  Pallas kernels  87 us (95%)
  local copies, waits for them, and re-layouts  2.76 us (3%)
  between operations  1.29 us (1%)
    pallas_call x1, Pallas kernels, admm(): pl.pallas_call(functools.partial(admm_kernel, sizes, offset, scale), in_s...  87 us

profile of v4, /device:TPU:1, one launch (start us, length us, event | category | flops | bytes accessed | tf_op | source)
XLA Modules:
  0.0 91.0 jit_solution(6071772625601432869)
XLA Ops:
  1.3 87.0 %admm.1 = f32[4,16,1024]{2,1,0:T(8,128)} custom-call(f32[1,1]{1,0:T(1,128)} %bitcast.21.penalty_hbm, bf16[8192,128]{1,0:T(8,128)(2,1)} %samples_hbm.1, bf16[64,8192]{1,0:T(8,128)(2,1)} %bitcast.22, s32[1,8192]{1,0:T(1,128)} %bitcast.26, bf16[128,1024]{1,0:T(8,128)(2,1)} %omega_hbm.1, f32[1,1024]{1,0:T(1,128)} %bitcast.27, f32[1024,1024]{1,0:T(8,128)} %factor_hbm.1, ...), custom_call_target="tpu_custom_call" | custom-call | tf_op jit(solution)/shard_map/admm/pallas_call | solution.py:535
  88.3 1.6 %slice_bitcast_fusion = (f32[1024,16]{0,1:T(8,128)}, f32[1024,16]{0,1:T(8,128)}, f32[1024,16]{0,1:T(8,128)}) fusion(f32[4,16,1024]{2,1,0:T(8,128)} %admm.1), kind=kLoop, calls=%fused_computation | loop fusion | bytes 393216 | tf_op jit(solution)/shard_map/transpose | solution.py:620
  89.8 1.2 %slice_bitcast_fusion.3 = f32[1,3]{1,0:T(1,128)} fusion(f32[4,16,1024]{2,1,0:T(8,128)} %admm.1), kind=kLoop, calls=%fused_computation.3 | loop fusion | bytes 24 | tf_op jit(solution)/shard_map/squeeze | solution.py:620

commit v5 on v4

--- a/solution.py
+++ b/solution.py
@@ -449,7 +449,7 @@
             total = rs_recv_ref[s, 0, :9]
             for r in range(1, n_region):
                 total = total + rs_recv_ref[s, r, :9]
-            mean_ref[s, region] = total[:8] / total[8:9]
+            mean_ref[s, region] = (total[:8] / total[8:9]).astype(BF16)
             mine = mean_ref.at[s, region]
             for k in region_order:
                 remote(mine, mine, mean_send.at[s], mean_recv.at[s], region_peer(k)).start()
@@ -458,7 +458,7 @@
             arrived(mean_ref.at[s, pl.ds(0, n_region - 1)], mean_recv.at[s])
             updated = jnp.concatenate(
                 [
-                    jnp.concatenate([mean_ref[s, h * lanes + j] for j in range(lanes)], axis=1)
+                    jnp.concatenate([mean_ref[s, h * lanes + j].astype(F32) for j in range(lanes)], axis=1)
                     for h in range(narrow // 8)
                 ],
                 axis=0,
@@ -563,7 +563,7 @@
             pltpu.VMEM((ITERS, PARTS) + part, BF16),
             pltpu.VMEM((ITERS, n_region, 16, 128), F32),
             pltpu.VMEM((ITERS, n_region, 16, 128), F32),
-            pltpu.VMEM((ITERS, n_region, 8, 128), F32),
+            pltpu.VMEM((ITERS, n_region, 8, 128), BF16),
             pltpu.VMEM((ITERS, group, 8, 128), F32),
             dma((10,)),
             dma((4,)),

time: 91.2 us -> 91.2 us (level)
  no operation moved by 1% of the time
where the time goes in v5:
time: 91.2 us; the launch traced here: 91 us
  Pallas kernels  86.9 us (95%)
  local copies, waits for them, and re-layouts  2.76 us (3%)
  between operations  1.29 us (1%)
    pallas_call x1, Pallas kernels, admm(): pl.pallas_call(functools.partial(admm_kernel, sizes, offset, scale), in_s...  86.9 us

profile of v5, /device:TPU:1, one launch (start us, length us, event | category | flops | bytes accessed | tf_op | source)
XLA Modules:
  0.0 91.0 jit_solution(5429483033805987340)
XLA Ops:
  1.3 86.9 %admm.1 = f32[4,16,1024]{2,1,0:T(8,128)} custom-call(f32[1,1]{1,0:T(1,128)} %bitcast.21.penalty_hbm, bf16[8192,128]{1,0:T(8,128)(2,1)} %samples_hbm.1, bf16[64,8192]{1,0:T(8,128)(2,1)} %bitcast.22, s32[1,8192]{1,0:T(1,128)} %bitcast.26, bf16[128,1024]{1,0:T(8,128)(2,1)} %omega_hbm.1, f32[1,1024]{1,0:T(1,128)} %bitcast.27, f32[1024,1024]{1,0:T(8,128)} %factor_hbm.1, ...), custom_call_target="tpu_custom_call" | custom-call | tf_op jit(solution)/shard_map/admm/pallas_call | solution.py:535
  88.2 1.6 %slice_bitcast_fusion = (f32[1024,16]{0,1:T(8,128)}, f32[1024,16]{0,1:T(8,128)}, f32[1024,16]{0,1:T(8,128)}) fusion(f32[4,16,1024]{2,1,0:T(8,128)} %admm.1), kind=kLoop, calls=%fused_computation | loop fusion | bytes 393216 | tf_op jit(solution)/shard_map/transpose | solution.py:620
  89.8 1.2 %slice_bitcast_fusion.3 = f32[1,3]{1,0:T(1,128)} fusion(f32[4,16,1024]{2,1,0:T(8,128)} %admm.1), kind=kLoop, calls=%fused_computation.3 | loop fusion | bytes 24 | tf_op jit(solution)/shard_map/squeeze | solution.py:620
